TPU v7x, 32 devices: a whole 2x2x4 slice. The times are simulated.
32 devices in a mesh: gx: 4 (over z), gy: 2 (over y), ea: 4 (over x, core).
Axes of the slice: x: 2, y: 2, z: 4, core: 2. Of those that a mesh axis runs over, the one named last changes fastest.
Arguments:
- load_displacement: float32 [3, 16, 32, 512], P(None, 'gx', 'gy', 'ea'), may hold values from -6 to 6
- load_enriched: float32 [15, 8192], P(None, ('gx', 'gy', 'ea')), may hold values from -24 to 24
- stiffness_shift: float32 [16, 32, 512], P('gx', 'gy', 'ea'), may hold values from 2 to 8
- enriched_diag: float32 [15, 8192], P(None, ('gx', 'gy', 'ea')), may hold values from 11 to 17
- enriched_off: float32 [15, 15, 8192], P(None, None, ('gx', 'gy', 'ea')), may hold values from -0.4 to 0.4
- coupling: float32 [3, 15, 16384], P(None, None, ('gx', 'gy', 'ea')), may hold values from -0.15 to 0.15
- slot_kind: int32 [32, 4, 128], P(('gx', 'gy', 'ea')), may hold values from 0 to 2, as said below
- slot_cell: int32 [32, 4, 128], P(('gx', 'gy', 'ea')), may hold values from 0 to 8191, as said below
- slot_node: int32 [32, 4, 128], P(('gx', 'gy', 'ea')), may hold values from 0 to 255, as said below
Outputs:
- solution_displacement: float32 [3, 16, 32, 512], P(None, 'gx', 'gy', 'ea')
- residual_displacement: float32 [3, 16, 32, 512], P(None, 'gx', 'gy', 'ea')
- solution_enriched: float32 [15, 8192], P(None, ('gx', 'gy', 'ea'))
- residual_enriched: float32 [15, 8192], P(None, ('gx', 'gy', 'ea'))
Inputs may be any that keep to these rules, and one draw needn't show every extreme that they name: `slot_kind`: within each block of 128 slots of one device to one owner the slots of kind 1 or 2 come first; in every draw some owner receives 128 such slots from each of the 4 devices of its column. `slot_cell`: distinct within one device. `slot_node`: distinct within each block of 128 slots of one device to one owner.
All inputs are finite; a program needn't handle non-finite values.
Results may differ from a plain program's by a relative error of at most 0.0003.
Values sent between devices are 32-bit elements; how exact they have to be, the bound alone decides.
A program may use at most 64 MiB of HBM per device.

v0:
```python
import functools

import jax
import jax.numpy as jnp
from jax import lax
from jax.experimental import pallas as pl
from jax.experimental.pallas import tpu as pltpu
from jax.sharding import PartitionSpec as P

ITERS = 3
CENTRE = 11.5
AXES = ("gx", "gy", "ea")
MESH = pl.DeviceIdType.MESH
F32 = jnp.float32
BF16 = jnp.bfloat16


def pieces(x):
    high = x.astype(BF16)
    return high, (x - high.astype(F32)).astype(BF16)


def dot_nn(x, onehot):
    high, low = pieces(x)
    return jnp.dot(high, onehot, preferred_element_type=F32) + jnp.dot(
        low, onehot, preferred_element_type=F32
    )


def nt(x, onehot):
    return lax.dot_general(x, onehot, (((1,), (1,)), ((), ())), preferred_element_type=F32)


def iota(shape, dim):
    return lax.broadcasted_iota(jnp.int32, shape, dim)


def cg_coefficients(moment):
    def inner(first, second):
        total = None
        for i, a in enumerate(first):
            for j, b in enumerate(second):
                term = a * b * moment[i + j]
                total = term if total is None else total + term
        return total

    one = jnp.ones_like(moment[0])
    residual, direction, solution = [one], [one], []
    norm = moment[0]
    for step in range(ITERS):
        image = [CENTRE * d for d in direction] + [0.0 * one]
        for i, d in enumerate(direction):
            image[i + 1] = image[i + 1] + d
        alpha = norm / inner(direction, image)
        solution = [
            (solution[i] if i < len(solution) else 0.0) + alpha * d
            for i, d in enumerate(direction)
        ]
        residual = [
            (residual[i] if i < len(residual) else 0.0) - alpha * d for i, d in enumerate(image)
        ]
        if step + 1 < ITERS:
            new = inner(residual, residual)
            ratio = new / norm
            norm = new
            direction = [
                r + (ratio * direction[i] if i < len(direction) else 0.0)
                for i, r in enumerate(residual)
            ]
    return solution, residual


def kernel(
    sizes, groups,
    load_v, load_w, shift, diag, off, coupling, kind, cell, node,
    sol_v, res_v, sol_w, res_w,
    vu, wu, weights, stiff, lanes, rows, rows_b, nodes_mine, nodes_recv, centre_diag,
    node_in, x_in, y_in, z_in, w_in, t_in, y_out, z_out, t_out, red, red_out,
    node_s, node_r, x_s, x_r, y_s, y_r, z_s, z_r, w_s, w_r, t_s, t_r, red_s, red_r,
):
    n_gx, n_gy, n_ea = sizes
    comps, dx, dy, dz = load_v.shape
    ecomp, enb = load_w.shape
    cap = node.shape[2]
    per = dx * dy
    allrows = comps * per
    groups8 = allrows // 8
    gi, gj, ek = (lax.axis_index(a) for a in AXES)
    own = {"gx": gi, "gy": gj, "ea": ek}
    count = dict(zip(AXES, sizes))

    def members(group):
        total = 1
        for a in group:
            total *= count[a]
        me = 0
        for a in group:
            me = me * count[a] + own[a]

        def target(d):
            flat = lax.rem(me + d, total)
            coords = dict(own)
            for a in reversed(group):
                coords[a] = lax.rem(flat, count[a])
                flat = lax.div(flat, count[a])
            return tuple(coords[a] for a in AXES)

        return total, me, target

    barrier = pltpu.get_barrier_semaphore()
    expected = 0
    for group in groups:
        total, _, target = members(group)
        for d in range(1, total):
            pl.semaphore_signal(barrier, inc=1, device_id=target(d), device_id_type=MESH)
        expected += total - 1

    vu[0] = load_v[...]
    wu[0] = load_w[...]
    for o in range(n_ea):
        c = cell[0, o : o + 1, :]
        row = lax.shift_right_logical(c, dz.bit_length() - 1) if dz & (dz - 1) == 0 else c // dz
        lane = c - row * dz
        lanes[o] = jnp.where(iota((dz, cap), 0) == lane, 1.0, 0.0).astype(BF16)
        r = jnp.where(iota((per, cap), 0) == row, 1.0, 0.0)
        rows[o] = r
        rows_b[o] = r.astype(BF16)
        nodes_mine[o] = jnp.where(
            iota((enb, cap), 0) == node[0, o : o + 1, :], 1.0, 0.0
        ).astype(BF16)
        k = kind[0, o : o + 1, :]
        heavi = jnp.where(k >= 1, 1.0, 0.0)
        tip = jnp.where(k == 2, 1.0, 0.0)
        mask = jnp.where(iota((ecomp, cap), 0) < 3, heavi, tip)
        for i in range(comps):
            weights[o, i] = coupling[i, :, o * cap : (o + 1) * cap] * mask
    centre_diag[...] = shift[...] + (6.0 - CENTRE)

    pl.semaphore_wait(barrier, expected)

    waits = []

    def send(src, dst, s_sem, r_sem, device):
        copy = pltpu.make_async_remote_copy(
            src_ref=src, dst_ref=dst, send_sem=s_sem, recv_sem=r_sem,
            device_id=device, device_id_type=MESH,
        )
        copy.start()
        return copy

    def partner(d):
        return lax.rem(ek + d, n_ea)

    has = {
        ("gx", 1): gi < n_gx - 1, ("gx", -1): gi > 0,
        ("gy", 1): gj < n_gy - 1, ("gy", -1): gj > 0,
        ("ea", 1): ek < n_ea - 1, ("ea", -1): ek > 0,
    }
    beside = {
        ("gx", s): (gi + s, gj, ek) for s in (1, -1)
    } | {("gy", s): (gi, gj + s, ek) for s in (1, -1)} | {
        ("ea", s): (gi, gj, ek + s) for s in (1, -1)
    }
    slot = {1: 0, -1: 1}

    def remote(src, dst, s_sem, r_sem, device):
        return pltpu.make_async_remote_copy(
            src_ref=src, dst_ref=dst, send_sem=s_sem, recv_sem=r_sem,
            device_id=device, device_id_type=MESH,
        )

    def x_copy(op, s):
        return remote(
            vu.at[op, :, dx - 1 if s == 1 else 0], x_in.at[op, slot[s]],
            x_s.at[op, slot[s]], x_r.at[op, slot[s]], beside["gx", s],
        )

    def y_copy(op, s):
        return remote(
            y_out.at[op, slot[s]], y_in.at[op, slot[s]],
            y_s.at[op, slot[s]], y_r.at[op, slot[s]], beside["gy", s],
        )

    def z_copy(op, s):
        return remote(
            z_out.at[op, slot[s]], z_in.at[op, slot[s]],
            z_s.at[op, slot[s]], z_r.at[op, slot[s]], beside["ea", s],
        )

    def w_copy(op, d):
        return remote(
            wu.at[op], w_in.at[op, ek], w_s.at[op, d], w_r.at[op, d], (gi, gj, partner(d))
        )

    def t_copy(op, d):
        return remote(
            t_out.at[op, partner(d)], t_in.at[op, ek], t_s.at[op, d], t_r.at[op, d],
            (gi, gj, partner(d)),
        )

    def node_copy(d):
        return remote(
            node, node_in.at[ek], node_s.at[d], node_r.at[d], (gi, gj, partner(d))
        )

    def nodes_onehot(tile_row):
        return jnp.where(iota((enb, cap), 0) == tile_row, 1.0, 0.0).astype(BF16)

    lane_i = iota((8, dz), 1)

    def product(op_a, op_b):
        pv = jnp.sum((vu[op_a] * vu[op_b]).reshape(groups8, 8, dz), axis=0)
        pw = jnp.sum(wu[op_a] * wu[op_b], axis=0, keepdims=True)
        row = jnp.sum(pv, axis=0, keepdims=True)
        total = row
        for b in range(enb // dz):
            total = total + pw[:, b * dz : (b + 1) * dz]
        return total

    moments = []
    for op in range(ITERS):
        for s in (1, -1):
            @pl.when(has["gx", s])
            def _():
                x_copy(op, s).start()
        for d in range(1, n_ea):
            w_copy(op, d).start()
            if op == 0:
                node_copy(d).start()
        v2 = vu[op].reshape(allrows, dz)
        for i in range(comps):
            for a in range(dx):
                at = i * dx + a
                y_out[op, 0, at : at + 1, :] = vu[op, i, a, dy - 1 : dy, :]
                y_out[op, 1, at : at + 1, :] = vu[op, i, a, 0:1, :]
        for s in (1, -1):
            @pl.when(has["gy", s])
            def _():
                y_copy(op, s).start()
        up = jnp.zeros((8, dz), F32)
        down = jnp.zeros((8, dz), F32)
        for g in range(groups8):
            part = v2[8 * g : 8 * g + 8]
            up = jnp.where(lane_i == g, part[:, dz - 1 : dz], up)
            down = jnp.where(lane_i == g, part[:, 0:1], down)
        z_out[op, 0] = up
        z_out[op, 1] = down
        for s in (1, -1):
            @pl.when(has["ea", s])
            def _():
                z_copy(op, s).start()
        high, low = pieces(v2)
        for o in range(n_ea):
            seen = jnp.dot(high, lanes[o], preferred_element_type=F32) + jnp.dot(
                low, lanes[o], preferred_element_type=F32
            )
            total = None
            for i in range(comps):
                picked = jnp.sum(
                    seen[i * per : (i + 1) * per] * rows[o], axis=0, keepdims=True
                )
                term = weights[o, i] * picked
                total = term if total is None else total + term
            t_out[op, o] = total
        for d in range(1, n_ea):
            t_copy(op, d).start()

        if op == 0:
            for p in range(ecomp):
                whole = 0.5 * (off[p] + off[:, p, :])
                stiff[p] = jnp.where(
                    iota((ecomp, enb), 0) == p, diag[p : p + 1, :] - CENTRE, whole
                )
            nodes_recv[ek] = nodes_mine[ek]
        v4 = vu[op]
        zero = jnp.zeros((comps, 1, dy, dz), F32)
        near = jnp.concatenate([zero, v4[:, : dx - 1]], axis=1) + jnp.concatenate(
            [v4[:, 1:], zero], axis=1
        )
        near = near.reshape(allrows, dz)
        lane_all = iota((allrows, dz), 1)
        row_all = lax.rem(iota((allrows, dz), 0), dy)
        near = near + jnp.where(lane_all == 0, 0.0, pltpu.roll(v2, 1, 1))
        near = near + jnp.where(lane_all == dz - 1, 0.0, pltpu.roll(v2, dz - 1, 1))
        near = near + jnp.where(row_all == 0, 0.0, pltpu.roll(v2, 1, 0))
        near = near + jnp.where(row_all == dy - 1, 0.0, pltpu.roll(v2, allrows - 1, 0))
        vu[op + 1] = centre_diag[...][None] * v4 - near.reshape(v4.shape)
        w = wu[op]
        acc = stiff[0] * w[0:1]
        for p in range(1, ecomp):
            acc = acc + stiff[p] * w[p : p + 1]
        if op == 0:
            moments.append(product(0, 0))
        else:
            moments.append(product(op, op))

        def to_cells(owner, w_owner):
            values = dot_nn(w_owner, nodes_mine[owner])
            spread_h, spread_l = [], []
            mask = rows_b[owner]
            for i in range(comps):
                term = jnp.sum(weights[owner, i] * values, axis=0, keepdims=True)
                h, l = pieces(term)
                spread_h.append(mask * h)
                spread_l.append(mask * l)
            place = lanes[owner]
            added = nt(jnp.concatenate(spread_h, axis=0), place) + nt(
                jnp.concatenate(spread_l, axis=0), place
            )
            vu[op + 1] += added.reshape(comps, dx, dy, dz)

        def to_nodes(source, terms):
            h, l = pieces(terms)
            onehot = nodes_recv[source]
            return nt(h, onehot) + nt(l, onehot)

        to_cells(ek, w)
        acc = acc + to_nodes(ek, t_out[op, ek])
        if op == 0:
            for d in range(1, n_ea):
                node_copy(d).wait_recv()
                source = lax.rem(ek + n_ea - d, n_ea)
                nodes_recv[source] = nodes_onehot(node_in[source, 0, pl.ds(ek, 1), :])
        for s in (1, -1):
            @pl.when(has["gx", -s])
            def _():
                x_copy(op, s).wait_recv()
                edge = 0 if s == 1 else dx - 1
                vu[op + 1, :, edge] -= x_in[op, slot[s]]

            @pl.when(has["gy", -s])
            def _():
                y_copy(op, s).wait_recv()
                edge = 0 if s == 1 else dy - 1
                for i in range(comps):
                    for a in range(dx):
                        at = i * dx + a
                        vu[op + 1, i, a, edge : edge + 1, :] -= y_in[op, slot[s], at : at + 1, :]

            @pl.when(has["ea", -s])
            def _():
                z_copy(op, s).wait_recv()
                edge = 0 if s == 1 else dz - 1
                tile = z_in[op, slot[s]]
                for i in range(comps):
                    for a in range(dx):
                        for b in range(dy // 8):
                            g = (i * dx + a) * (dy // 8) + b
                            vu[op + 1, i, a, 8 * b : 8 * b + 8, :] -= jnp.where(
                                lane_i == edge, tile[:, g : g + 1], 0.0
                            )
        for d in range(1, n_ea):
            source = lax.rem(ek + n_ea - d, n_ea)
            w_copy(op, d).wait_recv()
            to_cells(source, w_in[op, source])
        for d in range(1, n_ea):
            source = lax.rem(ek + n_ea - d, n_ea)
            t_copy(op, d).wait_recv()
            acc = acc + to_nodes(source, t_in[op, source])
        wu[op + 1] = acc
        moments.append(product(op, op + 1))

    lane_r = iota((1, dz), 1)
    packed = jnp.zeros((1, dz), F32)
    for n, row in enumerate(moments):
        packed = jnp.where(lane_r == n, jnp.sum(row, axis=1, keepdims=True), packed)
    for stage, group in enumerate(groups):
        total, me, target = members(group)
        red_out[stage] = packed

        def red_copy(d):
            return remote(
                red_out.at[stage], red.at[stage, me], red_s.at[stage, d], red_r.at[stage, d],
                target(d),
            )

        for d in range(1, total):
            red_copy(d).start()
        red[stage, me] = packed
        for d in range(1, total):
            red_copy(d).wait_recv()
        packed = jnp.sum(red[stage, :total], axis=0)

    sol, res = cg_coefficients([packed[:, n : n + 1] for n in range(2 * ITERS)])
    v_terms = [vu[n].reshape(allrows, dz) for n in range(ITERS + 1)]
    w_terms = [wu[n] for n in range(ITERS + 1)]

    def combine(coefs, terms):
        out = coefs[0] * terms[0]
        for c, t in zip(coefs[1:], terms[1:]):
            out = out + c * t
        return out

    sol_v[...] = combine(sol, v_terms).reshape(sol_v.shape)
    res_v[...] = combine(res, v_terms).reshape(res_v.shape)
    sol_w[...] = combine(sol, w_terms)
    res_w[...] = combine(res, w_terms)

    for op in range(ITERS):
        for s in (1, -1):
            @pl.when(has["gx", s])
            def _():
                x_copy(op, s).wait_send()

            @pl.when(has["gy", s])
            def _():
                y_copy(op, s).wait_send()

            @pl.when(has["ea", s])
            def _():
                z_copy(op, s).wait_send()
        for d in range(1, n_ea):
            w_copy(op, d).wait_send()
            t_copy(op, d).wait_send()
            if op == 0:
                node_copy(d).wait_send()
    for stage, group in enumerate(groups):
        total, me, target = members(group)
        for d in range(1, total):
            remote(
                red_out.at[stage], red.at[stage, me], red_s.at[stage, d], red_r.at[stage, d],
                target(d),
            ).wait_send()


def body(sizes, *args):
    load_v, load_w, shift, diag, off, coupling, kind, cell, node = args
    n_ea = sizes[2]
    total = sizes[0] * sizes[1] * sizes[2]
    groups = (AXES,) if total <= 64 else (("gx",), ("gy", "ea"))
    widest = total if total <= 64 else max(sizes[0], sizes[1] * sizes[2])
    comps, dx, dy, dz = load_v.shape
    ecomp, enb = load_w.shape
    cap = node.shape[2]
    vmem = pltpu.VMEM
    dma = pltpu.SemaphoreType.DMA
    y_rows = -(-comps * dx // 8) * 8
    scratch = [
        vmem((ITERS + 1, comps, dx, dy, dz), F32),
        vmem((ITERS + 1, ecomp, enb), F32),
        vmem((n_ea, comps, ecomp, cap), F32),
        vmem((ecomp, ecomp, enb), F32),
        vmem((n_ea, dz, cap), BF16),
        vmem((n_ea, dx * dy, cap), F32),
        vmem((n_ea, dx * dy, cap), BF16),
        vmem((n_ea, enb, cap), BF16),
        vmem((n_ea, enb, cap), BF16),
        vmem((dx, dy, dz), F32),
        vmem((n_ea,) + node.shape, jnp.int32),
        vmem((ITERS, 2, comps, dy, dz), F32),
        vmem((ITERS, 2, y_rows, dz), F32),
        vmem((ITERS, 2, 8, dz), F32),
        vmem((ITERS, n_ea, ecomp, enb), F32),
        vmem((ITERS, n_ea, ecomp, cap), F32),
        vmem((ITERS, 2, y_rows, dz), F32),
        vmem((ITERS, 2, 8, dz), F32),
        vmem((ITERS, n_ea, ecomp, cap), F32),
        vmem((len(groups), widest, 1, dz), F32),
        vmem((len(groups), 1, dz), F32),
        dma((n_ea,)), dma((n_ea,)),
        dma((ITERS, 2)), dma((ITERS, 2)),
        dma((ITERS, 2)), dma((ITERS, 2)),
        dma((ITERS, 2)), dma((ITERS, 2)),
        dma((ITERS, n_ea)), dma((ITERS, n_ea)),
        dma((ITERS, n_ea)), dma((ITERS, n_ea)),
        dma((len(groups), widest)), dma((len(groups), widest)),
    ]
    out = pl.pallas_call(
        functools.partial(kernel, sizes, groups),
        out_shape=(
            jax.ShapeDtypeStruct(load_v.shape, F32),
            jax.ShapeDtypeStruct(load_v.shape, F32),
            jax.ShapeDtypeStruct(load_w.shape, F32),
            jax.ShapeDtypeStruct(load_w.shape, F32),
        ),
        in_specs=[pl.BlockSpec(memory_space=vmem)] * 9,
        out_specs=[pl.BlockSpec(memory_space=vmem)] * 4,
        scratch_shapes=scratch,
        compiler_params=pltpu.CompilerParams(collective_id=0, has_side_effects=True),
        name="krylov",
    )(*args)
    return tuple(out)


def solution(mesh):
    column = ("gx", "gy", "ea")
    placed = (
        P(None, "gx", "gy", "ea"),
        P(None, column),
        P("gx", "gy", "ea"),
        P(None, column),
        P(None, None, column),
        P(None, None, column),
        P(column, None, None),
        P(column, None, None),
        P(column, None, None),
    )
    return jax.shard_map(
        functools.partial(body, tuple(mesh.shape[a] for a in AXES)),
        mesh=mesh,
        in_specs=placed,
        out_specs=(
            P(None, "gx", "gy", "ea"),
            P(None, "gx", "gy", "ea"),
            P(None, column),
            P(None, column),
        ),
        check_vma=False,
    )
```

profile of v0, /device:TPU:0, one launch (start us, length us, event | category | flops | bytes accessed | tf_op | source)
XLA Modules:
  0.0 30.9 jit_solution(12290653783297534037)
XLA Ops:
  0.6 26.7 %krylov.1 = (f32[3,4,16,128]{3,2,1,0:T(8,128)}, f32[3,4,16,128]{3,2,1,0:T(8,128)}, f32[15,256]{1,0:T(8,128)}, f32[15,256]{1,0:T(8,128)}) custom-call(f32[3,4,16,128]{3,2,1,0:T(8,128)} %load_v.1, f32[15,256]{1,0:T(8,128)} %load_w.1, f32[4,16,128]{2,1,0:T(8,128)} %shift.1, f32[15,256]{1,0:T(8,128)} %diag.1, f32[15,15,256]{2,1,0:T(8,128)} %off.1, ...), custom_call_target="tpu_custom_call" | custom-call | tf_op jit(solution)/shard_map/krylov/pallas_call | solution.py:468
  27.3 0.0 copy-start
  27.3 1.6 %copy.17 = f32[3,4,16,128]{3,2,1,0:T(8,128)} copy(f32[3,4,16,128]{3,2,1,0:T(8,128)} %get-tuple-element.8) | data formatting | bytes 196608
  28.9 0.0 copy-done
  28.9 0.0 copy-start.2
  28.9 0.6 %copy.18 = f32[3,4,16,128]{3,2,1,0:T(8,128)} copy(f32[3,4,16,128]{3,2,1,0:T(8,128)S(1)} %copy-done) | data formatting | bytes 196608
  29.5 0.1 copy-done.2
  29.6 0.0 copy-start.1
  29.6 0.6 %copy.19 = f32[15,256]{1,0:T(8,128)} copy(f32[15,256]{1,0:T(8,128)S(1)} %copy-done.2) | data formatting | bytes 30720
  30.2 0.1 copy-done.1
  30.3 0.6 %copy.20 = f32[15,256]{1,0:T(8,128)} copy(f32[15,256]{1,0:T(8,128)S(1)} %copy-done.1) | data formatting | bytes 30720
Async XLA Ops:
  27.3 1.6 %copy-start = (f32[3,4,16,128]{3,2,1,0:T(8,128)S(1)}, f32[3,4,16,128]{3,2,1,0:T(8,128)}, u32[]{:S(2)}) copy-start(f32[3,4,16,128]{3,2,1,0:T(8,128)} %get-tuple-element.9) | copy-start | bytes 294916
  28.9 0.7 %copy-start.2 = (f32[15,256]{1,0:T(8,128)S(1)}, f32[15,256]{1,0:T(8,128)}, u32[]{:S(2)}) copy-start(f32[15,256]{1,0:T(8,128)} %get-tuple-element.10) | copy-start | bytes 46084
  29.6 0.7 %copy-start.1 = (f32[15,256]{1,0:T(8,128)S(1)}, f32[15,256]{1,0:T(8,128)}, u32[]{:S(2)}) copy-start(f32[15,256]{1,0:T(8,128)} %get-tuple-element.11) | copy-start | bytes 46084
where the time goes:
time: 31.3 us; the launch traced here: 30.9 us
  Pallas kernels  26.7 us (85%)
  local copies, waits for them, and re-layouts  3.62 us (12%)
  between operations  0.65 us (2%)
    pallas_call x1, Pallas kernels, body(): pl.pallas_call(functools.partial(kernel, sizes, groups), out_shape=(jax.S...  26.7 us
    unnamed x10, local copies, waits for them, and re-layouts  3.62 us

commit v1 on v0

--- a/solution.py
+++ b/solution.py
@@ -20,15 +20,14 @@
     return high, (x - high.astype(F32)).astype(BF16)
 
 
-def dot_nn(x, onehot):
+def stacked(x):
     high, low = pieces(x)
-    return jnp.dot(high, onehot, preferred_element_type=F32) + jnp.dot(
-        low, onehot, preferred_element_type=F32
-    )
-
-
-def nt(x, onehot):
-    return lax.dot_general(x, onehot, (((1,), (1,)), ((), ())), preferred_element_type=F32)
+    return jnp.concatenate([high, low], axis=0)
+
+
+def folded(product):
+    half = product.shape[0] // 2
+    return product[:half] + product[half:]
 
 
 def iota(shape, dim):
@@ -72,15 +71,17 @@
 
 def kernel(
     sizes, groups,
-    load_v, load_w, shift, diag, off, coupling, kind, cell, node,
-    sol_v, res_v, sol_w, res_w,
-    vu, wu, weights, stiff, lanes, rows, rows_b, nodes_mine, nodes_recv, centre_diag,
+    load_v, load_w, shift_h, diag_h, off_h, coupling_h, kind_h, cell_h, node_h,
+    vu, wu, coefs,
+    w_first, shift, diag, off, coupling, kind, cell, node, load_s,
+    weights, stiff, lanes, lanes_t, rows, rows_b, nodes_mine, nodes_recv, centre_diag,
     node_in, x_in, y_in, z_in, w_in, t_in, y_out, z_out, t_out, red, red_out,
     node_s, node_r, x_s, x_r, y_s, y_r, z_s, z_r, w_s, w_r, t_s, t_r, red_s, red_r,
 ):
     n_gx, n_gy, n_ea = sizes
     comps, dx, dy, dz = load_v.shape
     ecomp, enb = load_w.shape
+    epad = wu.shape[1]
     cap = node.shape[2]
     per = dx * dy
     allrows = comps * per
@@ -115,38 +116,60 @@
             pl.semaphore_signal(barrier, inc=1, device_id=target(d), device_id_type=MESH)
         expected += total - 1
 
-    vu[0] = load_v[...]
-    wu[0] = load_w[...]
+    loads = {}
+    for at, (name, src, dst) in enumerate((
+        ("cell", cell_h, cell), ("v", load_v, vu.at[0]), ("node", node_h, node),
+        ("kind", kind_h, kind), ("w", load_w, w_first), ("coupling", coupling_h, coupling),
+        ("shift", shift_h, shift), ("off", off_h, off), ("diag", diag_h, diag),
+    )):
+        loads[name] = pltpu.make_async_copy(src, dst, load_s.at[at])
+        loads[name].start()
+
+    def columns(tile):
+        full = jnp.concatenate(
+            [tile.astype(F32), jnp.zeros((cap - tile.shape[0], cap), F32)], axis=0
+        )
+        return jnp.transpose(full).astype(jnp.int32)
+
+    loads["cell"].wait()
+    tile = cell[0]
+    tile_row = lax.div(tile, dz)
+    tile_lane = tile - tile_row * dz
+    lane_columns = columns(tile_lane)
     for o in range(n_ea):
-        c = cell[0, o : o + 1, :]
-        row = lax.shift_right_logical(c, dz.bit_length() - 1) if dz & (dz - 1) == 0 else c // dz
-        lane = c - row * dz
-        lanes[o] = jnp.where(iota((dz, cap), 0) == lane, 1.0, 0.0).astype(BF16)
-        r = jnp.where(iota((per, cap), 0) == row, 1.0, 0.0)
-        rows[o] = r
-        rows_b[o] = r.astype(BF16)
+        span = slice(o * cap, (o + 1) * cap)
+        lanes[:, span] = jnp.where(
+            iota((dz, cap), 0) == tile_lane[o : o + 1], 1.0, 0.0
+        ).astype(BF16)
+        lanes_t[span, :] = jnp.where(
+            iota((cap, dz), 1) == lane_columns[:, o : o + 1], 1.0, 0.0
+        ).astype(BF16)
+        r = jnp.where(iota((per, cap), 0) == tile_row[o : o + 1], 1.0, 0.0)
+        rows[:, span] = r
+        rows_b[:, span] = r.astype(BF16)
+    loads["node"].wait()
+    for o in range(n_ea):
         nodes_mine[o] = jnp.where(
             iota((enb, cap), 0) == node[0, o : o + 1, :], 1.0, 0.0
         ).astype(BF16)
-        k = kind[0, o : o + 1, :]
-        heavi = jnp.where(k >= 1, 1.0, 0.0)
-        tip = jnp.where(k == 2, 1.0, 0.0)
-        mask = jnp.where(iota((ecomp, cap), 0) < 3, heavi, tip)
-        for i in range(comps):
-            weights[o, i] = coupling[i, :, o * cap : (o + 1) * cap] * mask
-    centre_diag[...] = shift[...] + (6.0 - CENTRE)
+    loads["kind"].wait()
+    loads["coupling"].wait()
+    no_row = jnp.zeros((epad - ecomp, n_ea * cap), F32)
+    for i in range(comps):
+        for o in range(n_ea):
+            k = kind[0, o : o + 1, :]
+            heavi = jnp.where(k >= 1, 1.0, 0.0)
+            tip = jnp.where(k == 2, 1.0, 0.0)
+            mask = jnp.where(iota((ecomp, cap), 0) < 3, heavi, tip)
+            span = slice(o * cap, (o + 1) * cap)
+            weights[i, :, span] = jnp.concatenate(
+                [coupling[i, :, span] * mask, no_row[:, span]], axis=0
+            )
+    loads["w"].wait()
+    wu[0] = jnp.concatenate([w_first[...], jnp.zeros((epad - ecomp, enb), F32)], axis=0)
+    loads["v"].wait()
 
     pl.semaphore_wait(barrier, expected)
-
-    waits = []
-
-    def send(src, dst, s_sem, r_sem, device):
-        copy = pltpu.make_async_remote_copy(
-            src_ref=src, dst_ref=dst, send_sem=s_sem, recv_sem=r_sem,
-            device_id=device, device_id_type=MESH,
-        )
-        copy.start()
-        return copy
 
     def partner(d):
         return lax.rem(ek + d, n_ea)
@@ -203,10 +226,8 @@
             node, node_in.at[ek], node_s.at[d], node_r.at[d], (gi, gj, partner(d))
         )
 
-    def nodes_onehot(tile_row):
-        return jnp.where(iota((enb, cap), 0) == tile_row, 1.0, 0.0).astype(BF16)
-
     lane_i = iota((8, dz), 1)
+    lane_r = iota((1, dz), 1)
 
     def product(op_a, op_b):
         pv = jnp.sum((vu[op_a] * vu[op_b]).reshape(groups8, 8, dz), axis=0)
@@ -249,29 +270,31 @@
             @pl.when(has["ea", s])
             def _():
                 z_copy(op, s).start()
-        high, low = pieces(v2)
+        seen = folded(jnp.dot(stacked(v2), lanes[...], preferred_element_type=F32))
+        total = None
+        for i in range(comps):
+            picked = jnp.sum(seen[i * per : (i + 1) * per] * rows[...], axis=0, keepdims=True)
+            term = weights[i] * picked
+            total = term if total is None else total + term
         for o in range(n_ea):
-            seen = jnp.dot(high, lanes[o], preferred_element_type=F32) + jnp.dot(
-                low, lanes[o], preferred_element_type=F32
-            )
-            total = None
-            for i in range(comps):
-                picked = jnp.sum(
-                    seen[i * per : (i + 1) * per] * rows[o], axis=0, keepdims=True
-                )
-                term = weights[o, i] * picked
-                total = term if total is None else total + term
-            t_out[op, o] = total
+            t_out[op, o] = total[:, o * cap : (o + 1) * cap]
         for d in range(1, n_ea):
             t_copy(op, d).start()
 
         if op == 0:
+            loads["off"].wait()
+            loads["diag"].wait()
             for p in range(ecomp):
                 whole = 0.5 * (off[p] + off[:, p, :])
-                stiff[p] = jnp.where(
+                whole = jnp.where(
                     iota((ecomp, enb), 0) == p, diag[p : p + 1, :] - CENTRE, whole
                 )
-            nodes_recv[ek] = nodes_mine[ek]
+                stiff[p] = jnp.concatenate(
+                    [whole, jnp.zeros((epad - ecomp, enb), F32)], axis=0
+                )
+            loads["shift"].wait()
+            centre_diag[...] = shift[...] + (6.0 - CENTRE)
+            node_in[ek] = node[...]
         v4 = vu[op]
         zero = jnp.zeros((comps, 1, dy, dz), F32)
         near = jnp.concatenate([zero, v4[:, : dx - 1]], axis=1) + jnp.concatenate(
@@ -294,33 +317,44 @@
         else:
             moments.append(product(op, op))
 
-        def to_cells(owner, w_owner):
-            values = dot_nn(w_owner, nodes_mine[owner])
-            spread_h, spread_l = [], []
-            mask = rows_b[owner]
-            for i in range(comps):
-                term = jnp.sum(weights[owner, i] * values, axis=0, keepdims=True)
-                h, l = pieces(term)
-                spread_h.append(mask * h)
-                spread_l.append(mask * l)
-            place = lanes[owner]
-            added = nt(jnp.concatenate(spread_h, axis=0), place) + nt(
-                jnp.concatenate(spread_l, axis=0), place
-            )
-            vu[op + 1] += added.reshape(comps, dx, dy, dz)
-
-        def to_nodes(source, terms):
-            h, l = pieces(terms)
-            onehot = nodes_recv[source]
-            return nt(h, onehot) + nt(l, onehot)
-
-        to_cells(ek, w)
-        acc = acc + to_nodes(ek, t_out[op, ek])
+        w_in[op, ek] = w
+        t_in[op, ek] = t_out[op, ek]
+        if op + 1 == ITERS:
+            packed = jnp.zeros((1, dz), F32)
+            for n, row in enumerate(moments):
+                packed = jnp.where(lane_r == n, jnp.sum(row, axis=1, keepdims=True), packed)
         if op == 0:
             for d in range(1, n_ea):
                 node_copy(d).wait_recv()
-                source = lax.rem(ek + n_ea - d, n_ea)
-                nodes_recv[source] = nodes_onehot(node_in[source, 0, pl.ds(ek, 1), :])
+            own_rows = jnp.concatenate(
+                [node_in[o, 0, pl.ds(ek, 1), :] for o in range(n_ea)], axis=0
+            )
+            node_columns = columns(own_rows)
+            for o in range(n_ea):
+                nodes_recv[o * cap : (o + 1) * cap, :] = jnp.where(
+                    iota((cap, enb), 1) == node_columns[:, o : o + 1], 1.0, 0.0
+                ).astype(BF16)
+        for d in range(1, n_ea):
+            w_copy(op, d).wait_recv()
+        values = jnp.concatenate(
+            [
+                folded(jnp.dot(stacked(w_in[op, o]), nodes_mine[o], preferred_element_type=F32))
+                for o in range(n_ea)
+            ],
+            axis=1,
+        )
+        spread_h, spread_l = [], []
+        for i in range(comps):
+            h, l = pieces(jnp.sum(weights[i] * values, axis=0, keepdims=True))
+            spread_h.append(rows_b[...] * h)
+            spread_l.append(rows_b[...] * l)
+        added = folded(
+            jnp.dot(
+                jnp.concatenate(spread_h + spread_l, axis=0), lanes_t[...],
+                preferred_element_type=F32,
+            )
+        )
+        vu[op + 1] += added.reshape(comps, dx, dy, dz)
         for s in (1, -1):
             @pl.when(has["gx", -s])
             def _():
@@ -350,20 +384,16 @@
                                 lane_i == edge, tile[:, g : g + 1], 0.0
                             )
         for d in range(1, n_ea):
-            source = lax.rem(ek + n_ea - d, n_ea)
-            w_copy(op, d).wait_recv()
-            to_cells(source, w_in[op, source])
-        for d in range(1, n_ea):
-            source = lax.rem(ek + n_ea - d, n_ea)
             t_copy(op, d).wait_recv()
-            acc = acc + to_nodes(source, t_in[op, source])
+        terms = jnp.concatenate([t_in[op, o] for o in range(n_ea)], axis=1)
+        acc = acc + folded(
+            jnp.dot(stacked(terms), nodes_recv[...], preferred_element_type=F32)
+        )
         wu[op + 1] = acc
         moments.append(product(op, op + 1))
 
-    lane_r = iota((1, dz), 1)
-    packed = jnp.zeros((1, dz), F32)
-    for n, row in enumerate(moments):
-        packed = jnp.where(lane_r == n, jnp.sum(row, axis=1, keepdims=True), packed)
+    last = 2 * ITERS - 1
+    packed = jnp.where(lane_r == last, jnp.sum(moments[last], axis=1, keepdims=True), packed)
     for stage, group in enumerate(groups):
         total, me, target = members(group)
         red_out[stage] = packed
@@ -382,19 +412,10 @@
         packed = jnp.sum(red[stage, :total], axis=0)
 
     sol, res = cg_coefficients([packed[:, n : n + 1] for n in range(2 * ITERS)])
-    v_terms = [vu[n].reshape(allrows, dz) for n in range(ITERS + 1)]
-    w_terms = [wu[n] for n in range(ITERS + 1)]
-
-    def combine(coefs, terms):
-        out = coefs[0] * terms[0]
-        for c, t in zip(coefs[1:], terms[1:]):
-            out = out + c * t
-        return out
-
-    sol_v[...] = combine(sol, v_terms).reshape(sol_v.shape)
-    res_v[...] = combine(res, v_terms).reshape(res_v.shape)
-    sol_w[...] = combine(sol, w_terms)
-    res_w[...] = combine(res, w_terms)
+    tile = jnp.zeros((1, dz), F32)
+    for n, c in enumerate(sol + res):
+        tile = jnp.where(lane_r == n, c, tile)
+    coefs[...] = tile
 
     for op in range(ITERS):
         for s in (1, -1):
@@ -423,6 +444,28 @@
             ).wait_send()
 
 
+def combine_kernel(vu, wu, coefs, sol_v, res_v, sol_w, res_w):
+    ecomp = sol_w.shape[0]
+    tile = coefs[...]
+    solution = [tile[:, n : n + 1] for n in range(ITERS)]
+    residual = [tile[:, ITERS + n : ITERS + n + 1] for n in range(ITERS + 1)]
+
+    def combine(factors, terms):
+        out = factors[0] * terms[0]
+        for f, t in zip(factors[1:], terms[1:]):
+            out = out + f * t
+        return out
+
+    shape = sol_v.shape
+    flat = (shape[0] * shape[1] * shape[2], shape[3])
+    v_terms = [vu[n].reshape(flat) for n in range(ITERS + 1)]
+    w_terms = [wu[n] for n in range(ITERS + 1)]
+    sol_v[...] = combine(solution, v_terms).reshape(shape)
+    res_v[...] = combine(residual, v_terms).reshape(shape)
+    sol_w[...] = combine(solution, w_terms)[:ecomp]
+    res_w[...] = combine(residual, w_terms)[:ecomp]
+
+
 def body(sizes, *args):
     load_v, load_w, shift, diag, off, coupling, kind, cell, node = args
     n_ea = sizes[2]
@@ -435,26 +478,31 @@
     vmem = pltpu.VMEM
     dma = pltpu.SemaphoreType.DMA
     y_rows = -(-comps * dx // 8) * 8
+    epad = -(-ecomp // 16) * 16
+    slots = n_ea * cap
     scratch = [
-        vmem((ITERS + 1, comps, dx, dy, dz), F32),
-        vmem((ITERS + 1, ecomp, enb), F32),
-        vmem((n_ea, comps, ecomp, cap), F32),
-        vmem((ecomp, ecomp, enb), F32),
-        vmem((n_ea, dz, cap), BF16),
-        vmem((n_ea, dx * dy, cap), F32),
-        vmem((n_ea, dx * dy, cap), BF16),
+        vmem(load_w.shape, F32), vmem(shift.shape, F32), vmem(diag.shape, F32),
+        vmem(off.shape, F32), vmem(coupling.shape, F32),
+        vmem(kind.shape, jnp.int32), vmem(cell.shape, jnp.int32), vmem(node.shape, jnp.int32),
+        dma((9,)),
+        vmem((comps, epad, slots), F32),
+        vmem((ecomp, epad, enb), F32),
+        vmem((dz, slots), BF16),
+        vmem((slots, dz), BF16),
+        vmem((dx * dy, slots), F32),
+        vmem((dx * dy, slots), BF16),
         vmem((n_ea, enb, cap), BF16),
-        vmem((n_ea, enb, cap), BF16),
+        vmem((slots, enb), BF16),
         vmem((dx, dy, dz), F32),
         vmem((n_ea,) + node.shape, jnp.int32),
         vmem((ITERS, 2, comps, dy, dz), F32),
         vmem((ITERS, 2, y_rows, dz), F32),
         vmem((ITERS, 2, 8, dz), F32),
-        vmem((ITERS, n_ea, ecomp, enb), F32),
-        vmem((ITERS, n_ea, ecomp, cap), F32),
+        vmem((ITERS, n_ea, epad, enb), F32),
+        vmem((ITERS, n_ea, epad, cap), F32),
         vmem((ITERS, 2, y_rows, dz), F32),
         vmem((ITERS, 2, 8, dz), F32),
-        vmem((ITERS, n_ea, ecomp, cap), F32),
+        vmem((ITERS, n_ea, epad, cap), F32),
         vmem((len(groups), widest, 1, dz), F32),
         vmem((len(groups), 1, dz), F32),
         dma((n_ea,)), dma((n_ea,)),
@@ -465,21 +513,34 @@
         dma((ITERS, n_ea)), dma((ITERS, n_ea)),
         dma((len(groups), widest)), dma((len(groups), widest)),
     ]
-    out = pl.pallas_call(
+    basis = pl.pallas_call(
         functools.partial(kernel, sizes, groups),
         out_shape=(
-            jax.ShapeDtypeStruct(load_v.shape, F32),
-            jax.ShapeDtypeStruct(load_v.shape, F32),
-            jax.ShapeDtypeStruct(load_w.shape, F32),
-            jax.ShapeDtypeStruct(load_w.shape, F32),
+            pltpu.VMEM((ITERS + 1,) + load_v.shape, F32),
+            pltpu.VMEM((ITERS + 1, epad, enb), F32),
+            pltpu.VMEM((1, dz), F32),
         ),
-        in_specs=[pl.BlockSpec(memory_space=vmem)] * 9,
-        out_specs=[pl.BlockSpec(memory_space=vmem)] * 4,
+        in_specs=[pl.BlockSpec(memory_space=pltpu.HBM)] * 9,
+        out_specs=[pl.BlockSpec(memory_space=vmem)] * 3,
         scratch_shapes=scratch,
-        compiler_params=pltpu.CompilerParams(collective_id=0, has_side_effects=True),
+        compiler_params=pltpu.CompilerParams(
+            collective_id=0, has_side_effects=True
+        ),
         name="krylov",
     )(*args)
-    return tuple(out)
+    return tuple(
+        pl.pallas_call(
+            combine_kernel,
+            out_shape=tuple(
+                jax.ShapeDtypeStruct(like.shape, F32)
+                for like in (load_v, load_v, load_w, load_w)
+            ),
+            in_specs=[pl.BlockSpec(memory_space=vmem)] * 3,
+            out_specs=[pl.BlockSpec(memory_space=vmem)] * 4,
+            compiler_params=pltpu.CompilerParams(vmem_limit_bytes=8 << 20),
+            name="combine",
+        )(*basis)
+    )
 
 
 def solution(mesh):

time: 31.3 us -> 24.6 us (0.79)
  local copies, waits for them, and re-layouts: 3.62 us -> 0 us
  Pallas kernels: 26.7 us -> 23.8 us
    unnamed x10 -> x0, local copies, waits for them, and re-layouts: 3.62 us -> none
    pallas_call x1 -> x2, Pallas kernels: 26.7 us -> 23.8 us  [the longest x1 23 us: body(): pl.pallas_call(functools.partial(kernel, sizes, groups), out_shape=(pltpu...]
where the time goes in v1:
time: 24.6 us; the launch traced here: 24.5 us
  Pallas kernels  23.8 us (97%)
  between operations  0.64 us (3%)
    pallas_call x1, Pallas kernels, body(): pl.pallas_call(functools.partial(kernel, sizes, groups), out_shape=(pltpu...  23 us
    pallas_call x1, Pallas kernels, body(): pl.pallas_call(combine_kernel, out_shape=tuple((jax.ShapeDtypeStruct(like...  0.78 us

profile of v1, /device:TPU:0, one launch (start us, length us, event | category | flops | bytes accessed | tf_op | source)
XLA Modules:
  0.0 24.5 jit_solution(11840547472090305423)
XLA Ops:
  0.6 23.0 %krylov.1 = (f32[4,3,4,16,128]{4,3,2,1,0:T(8,128)S(1)}, f32[4,16,256]{2,1,0:T(8,128)S(1)}, f32[1,128]{1,0:T(1,128)S(1)}) custom-call(f32[3,4,16,128]{3,2,1,0:T(8,128)} %load_v.1, f32[15,256]{1,0:T(8,128)} %load_w.1, f32[4,16,128]{2,1,0:T(8,128)} %shift_h.1, f32[15,256]{1,0:T(8,128)} %diag_h.1, f32[15,15,256]{2,1,0:T(8,128)} %off_h.1, ...), custom_call_target="tpu_custom_call" | custom-call | tf_op jit(solution)/shard_map/krylov/pallas_call | solution.py:516
  23.7 0.8 %combine.1 = (f32[3,4,16,128]{3,2,1,0:T(8,128)}, f32[3,4,16,128]{3,2,1,0:T(8,128)}, f32[15,256]{1,0:T(8,128)}, f32[15,256]{1,0:T(8,128)}) custom-call(f32[4,3,4,16,128]{4,3,2,1,0:T(8,128)S(1)} %get-tuple-element.7.vu, f32[4,16,256]{2,1,0:T(8,128)S(1)} %get-tuple-element.8.wu, f32[1,128]{1,0:T(1,128)S(1)} %get-tuple-element.9.coefs), custom_call_target="tpu_custom_call" | custom-call | tf_op jit(solution)/shard_map/combine/pallas_call | solution.py:532

commit v2 on v1

--- a/solution.py
+++ b/solution.py
@@ -89,6 +89,9 @@
     gi, gj, ek = (lax.axis_index(a) for a in AXES)
     own = {"gx": gi, "gy": gj, "ea": ek}
     count = dict(zip(AXES, sizes))
+    wrapped = {
+        a: [own[a]] + [lax.rem(own[a] + d, count[a]) for d in range(1, count[a])] for a in AXES
+    }
 
     def members(group):
         total = 1
@@ -99,11 +102,10 @@
             me = me * count[a] + own[a]
 
         def target(d):
-            flat = lax.rem(me + d, total)
             coords = dict(own)
             for a in reversed(group):
-                coords[a] = lax.rem(flat, count[a])
-                flat = lax.div(flat, count[a])
+                coords[a] = wrapped[a][d % count[a]]
+                d //= count[a]
             return tuple(coords[a] for a in AXES)
 
         return total, me, target
@@ -135,23 +137,15 @@
     tile = cell[0]
     tile_row = lax.div(tile, dz)
     tile_lane = tile - tile_row * dz
-    lane_columns = columns(tile_lane)
     for o in range(n_ea):
         span = slice(o * cap, (o + 1) * cap)
         lanes[:, span] = jnp.where(
             iota((dz, cap), 0) == tile_lane[o : o + 1], 1.0, 0.0
         ).astype(BF16)
-        lanes_t[span, :] = jnp.where(
-            iota((cap, dz), 1) == lane_columns[:, o : o + 1], 1.0, 0.0
-        ).astype(BF16)
         r = jnp.where(iota((per, cap), 0) == tile_row[o : o + 1], 1.0, 0.0)
         rows[:, span] = r
         rows_b[:, span] = r.astype(BF16)
     loads["node"].wait()
-    for o in range(n_ea):
-        nodes_mine[o] = jnp.where(
-            iota((enb, cap), 0) == node[0, o : o + 1, :], 1.0, 0.0
-        ).astype(BF16)
     loads["kind"].wait()
     loads["coupling"].wait()
     no_row = jnp.zeros((epad - ecomp, n_ea * cap), F32)
@@ -172,7 +166,7 @@
     pl.semaphore_wait(barrier, expected)
 
     def partner(d):
-        return lax.rem(ek + d, n_ea)
+        return wrapped["ea"][d]
 
     has = {
         ("gx", 1): gi < n_gx - 1, ("gx", -1): gi > 0,
@@ -282,6 +276,14 @@
             t_copy(op, d).start()
 
         if op == 0:
+            lane_columns = columns(tile_lane)
+            for o in range(n_ea):
+                lanes_t[o * cap : (o + 1) * cap, :] = jnp.where(
+                    iota((cap, dz), 1) == lane_columns[:, o : o + 1], 1.0, 0.0
+                ).astype(BF16)
+                nodes_mine[o] = jnp.where(
+                    iota((enb, cap), 0) == node[0, o : o + 1, :], 1.0, 0.0
+                ).astype(BF16)
             loads["off"].wait()
             loads["diag"].wait()
             for p in range(ecomp):
@@ -334,27 +336,6 @@
                 nodes_recv[o * cap : (o + 1) * cap, :] = jnp.where(
                     iota((cap, enb), 1) == node_columns[:, o : o + 1], 1.0, 0.0
                 ).astype(BF16)
-        for d in range(1, n_ea):
-            w_copy(op, d).wait_recv()
-        values = jnp.concatenate(
-            [
-                folded(jnp.dot(stacked(w_in[op, o]), nodes_mine[o], preferred_element_type=F32))
-                for o in range(n_ea)
-            ],
-            axis=1,
-        )
-        spread_h, spread_l = [], []
-        for i in range(comps):
-            h, l = pieces(jnp.sum(weights[i] * values, axis=0, keepdims=True))
-            spread_h.append(rows_b[...] * h)
-            spread_l.append(rows_b[...] * l)
-        added = folded(
-            jnp.dot(
-                jnp.concatenate(spread_h + spread_l, axis=0), lanes_t[...],
-                preferred_element_type=F32,
-            )
-        )
-        vu[op + 1] += added.reshape(comps, dx, dy, dz)
         for s in (1, -1):
             @pl.when(has["gx", -s])
             def _():
@@ -384,7 +365,27 @@
                                 lane_i == edge, tile[:, g : g + 1], 0.0
                             )
         for d in range(1, n_ea):
+            w_copy(op, d).wait_recv()
             t_copy(op, d).wait_recv()
+        values = jnp.concatenate(
+            [
+                folded(jnp.dot(stacked(w_in[op, o]), nodes_mine[o], preferred_element_type=F32))
+                for o in range(n_ea)
+            ],
+            axis=1,
+        )
+        spread_h, spread_l = [], []
+        for i in range(comps):
+            h, l = pieces(jnp.sum(weights[i] * values, axis=0, keepdims=True))
+            spread_h.append(rows_b[...] * h)
+            spread_l.append(rows_b[...] * l)
+        added = folded(
+            jnp.dot(
+                jnp.concatenate(spread_h + spread_l, axis=0), lanes_t[...],
+                preferred_element_type=F32,
+            )
+        )
+        vu[op + 1] += added.reshape(comps, dx, dy, dz)
         terms = jnp.concatenate([t_in[op, o] for o in range(n_ea)], axis=1)
         acc = acc + folded(
             jnp.dot(stacked(terms), nodes_recv[...], preferred_element_type=F32)

time: 24.6 us -> 24.9 us (1.012)
  Pallas kernels: 23.8 us -> 24.1 us
    pallas_call x1, Pallas kernels: 23 us -> 23.3 us  [body(): pl.pallas_call(functools.partial(kernel, sizes, groups), out_shape=(pltpu...]
where the time goes in v2:
time: 24.9 us; the launch traced here: 24.7 us
  Pallas kernels  24.1 us (97%)
  between operations  0.64 us (3%)
    pallas_call x1, Pallas kernels, body(): pl.pallas_call(functools.partial(kernel, sizes, groups), out_shape=(pltpu...  23.3 us
    pallas_call x1, Pallas kernels, body(): pl.pallas_call(combine_kernel, out_shape=tuple((jax.ShapeDtypeStruct(like...  0.78 us

profile of v2, /device:TPU:0, one launch (start us, length us, event | category | flops | bytes accessed | tf_op | source)
XLA Modules:
  0.0 24.7 jit_solution(1409680807474748167)
XLA Ops:
  0.6 23.3 %krylov.1 = (f32[4,3,4,16,128]{4,3,2,1,0:T(8,128)S(1)}, f32[4,16,256]{2,1,0:T(8,128)S(1)}, f32[1,128]{1,0:T(1,128)S(1)}) custom-call(f32[3,4,16,128]{3,2,1,0:T(8,128)} %load_v.1, f32[15,256]{1,0:T(8,128)} %load_w.1, f32[4,16,128]{2,1,0:T(8,128)} %shift_h.1, f32[15,256]{1,0:T(8,128)} %diag_h.1, f32[15,15,256]{2,1,0:T(8,128)} %off_h.1, ...), custom_call_target="tpu_custom_call" | custom-call | tf_op jit(solution)/shard_map/krylov/pallas_call | solution.py:517
  24.0 0.8 %combine.1 = (f32[3,4,16,128]{3,2,1,0:T(8,128)}, f32[3,4,16,128]{3,2,1,0:T(8,128)}, f32[15,256]{1,0:T(8,128)}, f32[15,256]{1,0:T(8,128)}) custom-call(f32[4,3,4,16,128]{4,3,2,1,0:T(8,128)S(1)} %get-tuple-element.7.vu, f32[4,16,256]{2,1,0:T(8,128)S(1)} %get-tuple-element.8.wu, f32[1,128]{1,0:T(1,128)S(1)} %get-tuple-element.9.coefs), custom_call_target="tpu_custom_call" | custom-call | tf_op jit(solution)/shard_map/combine/pallas_call | solution.py:533
